TPU v7x, 32 devices: a whole 2x2x4 slice. The times are simulated.
32 devices in a mesh: ctx: 8 (over z, x), rep: 4 (over y, core).
Axes of the slice: x: 2, y: 2, z: 4, core: 2. Of those that a mesh axis runs over, the one named last changes fastest.
Arguments:
- latents: bfloat16 [131072, 576], P(('ctx', 'rep')), may hold values from -6 to 6
- queries: bfloat16 [64, 73728], P('rep', 'ctx'), may hold values from -4000 to 4000, as said below
- hot_ids: int32 [16], P('ctx'), may hold values from 0 to 15, as said below
- lengths: int32 [64], P('rep'), may hold values from 65536 to 131072
Outputs:
- attended: bfloat16 [64, 65536], P('rep', 'ctx')
Inputs may be any that keep to these rules, and one draw needn't show every extreme that they name: `queries`: query entries lie in the stated range. `hot_ids`: entries g * 2 to (g + 1) * 2 - 1 are distinct block numbers within group g.
All inputs are finite; a program needn't handle non-finite values.
Results may differ from a plain program's by a relative error of at most 0.0031.
Values may be sent and summed in bfloat16 or wider, within the bound.
A program may use at most 128 MiB of HBM per device.

v0:
```python
import jax
import jax.numpy as jnp
from jax import lax
from jax.sharding import PartitionSpec as P

H = 128
LAT = 512
ROPE = 64
QK = 192
BLK = 1024
HOT_GRP = 2


def from_root(block, axis, holder):
    block = jnp.where(lax.axis_index(axis) == holder, block, jnp.zeros_like(block))
    return lax.psum(block, axis)


def on_device(latents, queries, hot_ids, lengths):
    row_width = LAT + ROPE
    score_scale = QK ** (-0.5)
    rep_count = lax.axis_size("rep")
    group_index = lax.axis_index("ctx")
    per_device = latents.shape[0] // BLK
    blocks_held = []
    for slot_index in range(HOT_GRP):
        owner_index = hot_ids[slot_index] // per_device
        local_block = lax.dynamic_slice_in_dim(
            latents, hot_ids[slot_index] % per_device * BLK, BLK, 0
        )
        blocks_held.append(from_root(local_block, "rep", owner_index))
    key_rows = jnp.concatenate(blocks_held, axis=0)
    value_rows = key_rows[:, :LAT]
    offsets = jnp.arange(BLK, dtype=jnp.int32)
    row_index = (
        (group_index * (rep_count * per_device) + hot_ids)[:, None] * BLK + offsets[None, :]
    ).reshape(-1)
    all_heads = lax.all_gather(queries, "ctx", axis=1, tiled=True)
    query_count = all_heads.shape[0]
    query_blocks = all_heads.reshape(query_count // 4, 4, H, row_width)
    span_blocks = lengths.reshape(query_count // 4, 4)

    def partial_value(item_pair):
        query_block, span_block = item_pair
        scores = (
            jnp.einsum("qhw,kw->qhk", query_block, key_rows, preferred_element_type=jnp.float32)
            * score_scale
        )
        visible = row_index[None, None, :] < span_block[:, None, None]
        peak_score = jnp.max(jnp.where(visible, scores, -1e30), axis=2)
        exponent = jnp.where(visible, scores - peak_score[:, :, None], -1e30)
        weights = jnp.exp(exponent).astype(jnp.bfloat16)
        totals = jnp.sum(weights, axis=2, dtype=jnp.float32)
        numerators = jnp.einsum(
            "qhk,kl->qhl", weights, value_rows, preferred_element_type=jnp.float32
        )
        return (numerators, peak_score, totals)

    numerators, peak_score, totals = lax.map(partial_value, (query_blocks, span_blocks))
    numerators = numerators.reshape(query_count, H, LAT)
    peak_score = peak_score.reshape(query_count, H)
    totals = totals.reshape(query_count, H)
    all_numer, all_peak, all_total = (
        lax.all_to_all(numerators[None], "ctx", split_axis=2, concat_axis=0, tiled=True),
        lax.all_to_all(peak_score[None], "ctx", split_axis=2, concat_axis=0, tiled=True),
        lax.all_to_all(totals[None], "ctx", split_axis=2, concat_axis=0, tiled=True),
    )
    overall = jnp.max(all_peak, axis=0)
    factor = jnp.exp(all_peak - overall[None])
    merged = jnp.sum(all_numer * factor[..., None], axis=0)
    weight_sum = jnp.sum(all_total * factor, axis=0)
    return (merged / weight_sum[..., None]).reshape(query_count, -1).astype(jnp.bfloat16)


def solution(mesh):
    placed = (P(("ctx", "rep"), None), P("rep", "ctx"), P("ctx"), P("rep"))
    return jax.shard_map(
        on_device, mesh=mesh, in_specs=placed, out_specs=P("rep", "ctx"), check_vma=False
    )
```

profile of v0, /device:TPU:0, one launch (start us, length us, event | category | flops | bytes accessed | tf_op | source)
XLA Modules:
  0.0 254.2 jit_solution(5459596877738601110)
XLA Ops:
  7.4 1.4 fusion.19
  13.9 3.7 %dynamic-slice_select_fusion = (bf16[1024,576]{0,1:T(8,128)(2,1)}, bf16[1024,576]{0,1:T(8,128)(2,1)}) fusion(bf16[4096,576]{0,1:T(8,128)(2,1)} %param.6, s32[]{:T(128)S(6)} %select_n.53, pred[]{:T(512)S(6)} %eq.10, s32[]{:T(128)S(6)} %select_n.48, pred[]{:T(512)S(6)} %eq.9), kind=kLoop, calls=%fused_computation.23 | loop fusion | flops 1179648 | bytes 4718602 | tf_op jit(solution)/shard_map/jit(_where)/select_n | solution.py:15
  18.3 57.9 %all-reduce.3.cloned.1.call-done = (bf16[1024,576]{0,1:T(8,128)(2,1)}, bf16[1024,576]{0,1:T(8,128)(2,1)}) async-done(((bf16[1024,576]{0,1:T(8,128)(2,1)}, bf16[1024,576]{0,1:T(8,128)(2,1)}), (bf16[1024,576]{0,1:T(8,128)(2,1)}, bf16[1024,576]{0,1:T(8,128)(2,1)})) %all-reduce.3.cloned.1.call-update) | async-done | bytes 2359312 | tf_op jit(solution)/shard_map/psum | solution.py:16
  76.1 1.4 constant_dynamic-update-slice_fusion.1
  77.5 1.4 constant_dynamic-update-slice_fusion
  78.9 1.5 slice.14
  80.4 3.9 %copy.30 = bf16[2048,512]{1,0:T(8,128)(2,1)} copy(bf16[2048,512]{0,1:T(8,128)(2,1)} %slice.14) | data formatting | bytes 4194304
  84.3 5.5 %reshape.58 = bf16[4,4,128,576]{3,2,1,0:T(8,128)(2,1)} reshape(bf16[16,73728]{1,0:T(8,128)(2,1)} %all-gather.2.cloned.1.call-done) | data formatting | bytes 4718592 | tf_op jit(solution)/shard_map/reshape | solution.py:40
  89.8 4.4 %copy.24 = bf16[4,4,128,576]{2,3,1,0:T(8,128)(2,1)} copy(bf16[4,4,128,576]{3,2,1,0:T(8,128)(2,1)} %reshape.58) | data formatting | bytes 4718592
  94.2 27.9 %while.15 = (s32[]{:T(128)}, f32[4,4,128,512]{3,2,1,0:T(8,128)}, f32[4,4,128]{2,1,0:T(4,128)S(1)}, f32[4,4,128]{2,1,0:T(4,128)S(1)}, s32[4,4]{1,0:T(4,128)S(1)},...) while((s32[]{:T(128)}, f32[4,4,128,512]{3,2,1,0:T(8,128)}, ...), condition=%wide.region_5.6_spmd.clone, body=%wide.region_2.5_spmd.clone.sunk | while | flops 2295342080 | bytes 27149504 | solution.py:59
  94.4 3.4 %select_reduce_fusion.2 = (f32[4,128]{1,0:T(4,128)S(1)}, f32[4,128,2048]{2,1,0:T(8,128)S(1)}) fusion(pred[4,2048]{1,0:T(4,128)(4,1)S(1)} %broadcast_compare_fusion.2, bf16[2048,576]{0,1:T(8,128)(2,1)S(1)} %get-tuple-element.242, bf16[4,4,128,576]{2,3,1,0:T(8,128)(2,1)} %get-tuple-element.241, s32[]{:T(128)} %get-tuple-element.226), kind=kOutput, calls=%fused_computation.3.clone.1 | convolution fusion | flops 1211104768 | bytes 7154176 | tf_op jit(solution)/shard_map/while/body/eval_jaxpr/qhw,kw->qhk/dot_general | solution.py:46
  97.7 1.1 convert_reduce_fusion.2
  98.8 2.3 fusion.25
  101.3 3.4 %select_reduce_fusion.2 = (f32[4,128]{1,0:T(4,128)S(1)}, f32[4,128,2048]{2,1,0:T(8,128)S(1)}) fusion(pred[4,2048]{1,0:T(4,128)(4,1)S(1)} %broadcast_compare_fusion.2, bf16[2048,576]{0,1:T(8,128)(2,1)S(1)} %get-tuple-element.242, bf16[4,4,128,576]{2,3,1,0:T(8,128)(2,1)} %get-tuple-element.241, s32[]{:T(128)} %get-tuple-element.226), kind=kOutput, calls=%fused_computation.3.clone.1 | convolution fusion | flops 1211104768 | bytes 7154176 | tf_op jit(solution)/shard_map/while/body/eval_jaxpr/qhw,kw->qhk/dot_general | solution.py:46
  104.7 1.1 convert_reduce_fusion.2
  105.8 2.4 fusion.25
  108.3 3.4 %select_reduce_fusion.2 = (f32[4,128]{1,0:T(4,128)S(1)}, f32[4,128,2048]{2,1,0:T(8,128)S(1)}) fusion(pred[4,2048]{1,0:T(4,128)(4,1)S(1)} %broadcast_compare_fusion.2, bf16[2048,576]{0,1:T(8,128)(2,1)S(1)} %get-tuple-element.242, bf16[4,4,128,576]{2,3,1,0:T(8,128)(2,1)} %get-tuple-element.241, s32[]{:T(128)} %get-tuple-element.226), kind=kOutput, calls=%fused_computation.3.clone.1 | convolution fusion | flops 1211104768 | bytes 7154176 | tf_op jit(solution)/shard_map/while/body/eval_jaxpr/qhw,kw->qhk/dot_general | solution.py:46
  111.7 1.1 convert_reduce_fusion.2
  112.8 2.3 fusion.25
  115.3 3.4 %select_reduce_fusion.2 = (f32[4,128]{1,0:T(4,128)S(1)}, f32[4,128,2048]{2,1,0:T(8,128)S(1)}) fusion(pred[4,2048]{1,0:T(4,128)(4,1)S(1)} %broadcast_compare_fusion.2, bf16[2048,576]{0,1:T(8,128)(2,1)S(1)} %get-tuple-element.242, bf16[4,4,128,576]{2,3,1,0:T(8,128)(2,1)} %get-tuple-element.241, s32[]{:T(128)} %get-tuple-element.226), kind=kOutput, calls=%fused_computation.3.clone.1 | convolution fusion | flops 1211104768 | bytes 7154176 | tf_op jit(solution)/shard_map/while/body/eval_jaxpr/qhw,kw->qhk/dot_general | solution.py:46
  118.6 1.1 convert_reduce_fusion.2
  119.8 2.3 fusion.25
  122.7 0.7 reduce.3
  124.1 5.5 %all-to-all-start.1 = ((f32[8,1,256]{2,1,0:T(1,128)}), f32[8,1,256]{2,1,0:T(1,128)S(1)}, u32[]{:S(2)}, u32[]{:S(2)}) async-start(f32[8,1,256]{2,1,0:T(1,128)} %reshape.61), calls=%async_computation.1 | async-start | bytes 16384 | tf_op jit(solution)/shard_map/all_to_all | solution.py:65
  129.7 0.7 reduce.1
  131.1 5.0 %all-to-all-done.1 = f32[8,1,256]{2,1,0:T(1,128)S(1)} async-done(((f32[8,1,256]{2,1,0:T(1,128)}), f32[8,1,256]{2,1,0:T(1,128)S(1)}, u32[]{:S(2)}, u32[]{:S(2)}) %all-to-all-start.1) | async-done | bytes 8224 | tf_op jit(solution)/shard_map/all_to_all | solution.py:65
  136.1 3.3 %all-to-all-start.2 = ((f32[8,1,256]{2,1,0:T(1,128)}), f32[8,1,256]{2,1,0:T(1,128)S(1)}, u32[]{:S(2)}, u32[]{:S(2)}) async-start(f32[8,1,256]{2,1,0:T(1,128)} %reshape.63), calls=%async_computation.2 | async-start | bytes 16384 | tf_op jit(solution)/shard_map/all_to_all | solution.py:66
  139.5 6.6 %copy.29 = f32[1,16,128,512]{3,1,0,2:T(8,128)} copy(f32[1,16,128,512]{3,2,1,0:T(8,128)} %bitcast.2) | data formatting | bytes 8388608 | tf_op jit(solution)/shard_map/broadcast_in_dim;reshape | solution.py:64
  146.1 5.9 %all-to-all-start = ((f32[1,16,128,512]{3,1,0,2:T(8,128)}), f32[1,16,128,512]{3,1,0,2:T(8,128)}, u32[]{:S(2)}, u32[]{:S(2)}) async-start(f32[1,16,128,512]{3,1,0,2:T(8,128)} %copy.29), calls=%async_computation | async-start | bytes 8388608 | tf_op jit(solution)/shard_map/all_to_all | solution.py:64
  153.5 89.8 %all-to-all-done = f32[1,16,128,512]{3,1,0,2:T(8,128)} async-done(((f32[1,16,128,512]{3,1,0,2:T(8,128)}), f32[1,16,128,512]{3,1,0,2:T(8,128)}, u32[]{:S(2)}, u32[]{:S(2)}) %all-to-all-start) | async-done | bytes 4194336 | tf_op jit(solution)/shard_map/all_to_all | solution.py:64
  243.3 2.6 %multiply_reduce_fusion = f32[16,16,512]{2,0,1:T(8,128)S(1)} fusion(f32[8,16,16,512]{3,1,2,0:T(8,128)} %bitcast.5, f32[8,16,16]{1,2,0:T(8,128)S(1)} %get-tuple-element.144), kind=kLoop, calls=%fused_computation.22 | loop fusion | flops 1966080 | bytes 4726784 | tf_op jit(solution)/shard_map/reduce_sum | solution.py:70
  246.0 0.7 copy.32
  (55 shorter events, 5.1 us)
Async XLA Ops:
  7.4 10.9 %copy-start.1 = (s32[2]{0:T(128)S(1)}, s32[2]{0:T(128)}, u32[]{:S(2)}) copy-start(s32[2]{0:T(128)} %param.8) | copy-start | bytes 28
  7.4 10.8 %copy-start.2 = (s32[16]{0:T(128)S(1)}, s32[16]{0:T(128)}, u32[]{:S(2)}) copy-start(s32[16]{0:T(128)} %param.9) | copy-start | bytes 196
  7.4 68.8 %all-reduce.3.cloned.1.call-start = ((), (), s32[]{:S(2)}) async-start(), calls=%async_computation.4 | async-start | bytes 4718592 | tf_op jit(solution)/shard_map/psum | solution.py:16
  17.6 66.7 %all-gather.2.cloned.1.call-start = ((), (), s32[]{:S(2)}) async-start(), calls=%async_computation.3 | async-start | bytes 2654208 | tf_op jit(solution)/shard_map/all_gather | solution.py:38
  94.4 4.5 %copy-start = (bf16[2048,512]{1,0:T(8,128)(2,1)S(1)}, bf16[2048,512]{1,0:T(8,128)(2,1)}, u32[]{:S(2)}) copy-start(bf16[2048,512]{1,0:T(8,128)(2,1)} %get-tuple-element.243) | copy-start | bytes 6291460 | tf_op jit(solution)/shard_map/while
  101.3 4.5 %copy-start = (bf16[2048,512]{1,0:T(8,128)(2,1)S(1)}, bf16[2048,512]{1,0:T(8,128)(2,1)}, u32[]{:S(2)}) copy-start(bf16[2048,512]{1,0:T(8,128)(2,1)} %get-tuple-element.243) | copy-start | bytes 6291460 | tf_op jit(solution)/shard_map/while
  108.3 4.5 %copy-start = (bf16[2048,512]{1,0:T(8,128)(2,1)S(1)}, bf16[2048,512]{1,0:T(8,128)(2,1)}, u32[]{:S(2)}) copy-start(bf16[2048,512]{1,0:T(8,128)(2,1)} %get-tuple-element.243) | copy-start | bytes 6291460 | tf_op jit(solution)/shard_map/while
  115.3 4.5 %copy-start = (bf16[2048,512]{1,0:T(8,128)(2,1)S(1)}, bf16[2048,512]{1,0:T(8,128)(2,1)}, u32[]{:S(2)}) copy-start(bf16[2048,512]{1,0:T(8,128)(2,1)} %get-tuple-element.243) | copy-start | bytes 6291460 | tf_op jit(solution)/shard_map/while
  124.1 12.0 %all-to-all-start.1 = ((f32[8,1,256]{2,1,0:T(1,128)}), f32[8,1,256]{2,1,0:T(1,128)S(1)}, u32[]{:S(2)}, u32[]{:S(2)}) async-start(f32[8,1,256]{2,1,0:T(1,128)} %reshape.61), calls=%async_computation.1 | async-start | bytes 16384 | tf_op jit(solution)/shard_map/all_to_all | solution.py:65
  136.1 9.9 %all-to-all-start.2 = ((f32[8,1,256]{2,1,0:T(1,128)}), f32[8,1,256]{2,1,0:T(1,128)S(1)}, u32[]{:S(2)}, u32[]{:S(2)}) async-start(f32[8,1,256]{2,1,0:T(1,128)} %reshape.63), calls=%async_computation.2 | async-start | bytes 16384 | tf_op jit(solution)/shard_map/all_to_all | solution.py:66
  146.1 97.3 %all-to-all-start = ((f32[1,16,128,512]{3,1,0,2:T(8,128)}), f32[1,16,128,512]{3,1,0,2:T(8,128)}, u32[]{:S(2)}, u32[]{:S(2)}) async-start(f32[1,16,128,512]{3,1,0,2:T(8,128)} %copy.29), calls=%async_computation | async-start | bytes 8388608 | tf_op jit(solution)/shard_map/all_to_all | solution.py:64
Sparse Core Ops, SparseCore 0:
  17.7 58.3 all-reduce.2
Sparse Core Ops, SparseCore 1:
  20.3 54.4 all-gather.1
where the time goes:
time: 255 us; the launch traced here: 254 us
  waiting for transfers between devices  153 us (60%)
  local copies, waits for them, and re-layouts  29.3 us (11%)
  matrix products  22.7 us (9%)
  between operations  20 us (8%)
  starting transfers between devices  14.8 us (6%)
  other arithmetic  14 us (5%)
    all_to_all x1, waiting for transfers between devices, on_device(): lax.all_to_all(numerators[None], 'ctx', split_axis=2, concat_axis=0, tile...  89.8 us
    psum x1, waiting for transfers between devices, from_root(): return lax.psum(block, axis)  57.9 us
    dot_general x4, matrix products, partial_value(): jnp.einsum('qhw,kw->qhk', query_block, key_rows, preferred_element_type=j...  13.4 us
    unnamed x12, local copies, waits for them, and re-layouts  11.9 us
    dot_general x4, matrix products, partial_value(): jnp.einsum('qhk,kl->qhl', weights, value_rows, preferred_element_type=jnp...  9.3 us
    another operation x1, local copies, waits for them, and re-layouts, on_device(): numerators[None]  6.59 us
    all_to_all x1, starting transfers between devices, on_device(): lax.all_to_all(numerators[None], 'ctx', split_axis=2, concat_axis=0, tile...  5.93 us
    all_to_all x1, starting transfers between devices, on_device(): lax.all_to_all(peak_score[None], 'ctx', split_axis=2, concat_axis=0, tile...  5.51 us
  transfers between devices with their start and end apart: 5, of which 3 were waited for; matrix products, arithmetic and copies ran while one was open for 7% of the time, Pallas kernels for 0%

commit v1 on v0

--- a/solution.py
+++ b/solution.py
@@ -13,7 +13,7 @@
 
 def from_root(block, axis, holder):
     block = jnp.where(lax.axis_index(axis) == holder, block, jnp.zeros_like(block))
-    return lax.psum(block, axis)
+    return jnp.sum(lax.all_gather(block, axis), axis=0)
 
 
 def on_device(latents, queries, hot_ids, lengths):

time: 255 us -> 326 us (1.28)
  waiting for transfers between devices: 153 us -> 194 us
  other arithmetic: 14 us -> 33.9 us
  local copies, waits for them, and re-layouts: 29.3 us -> 40.9 us
    psum x1 -> x0, waiting for transfers between devices: 57.9 us -> none  [from_root(): return lax.psum(block, axis)]
    all_gather x0 -> x2, waiting for transfers between devices: none -> 51.9 us  [from_root(): return jnp.sum(lax.all_gather(block, axis), axis=0)]
    all_gather x1, waiting for transfers between devices: 0.01 us -> 45.4 us  [on_device(): all_heads = lax.all_gather(queries, 'ctx', axis=1, tiled=True)]
    all_gather x0 -> x2, local copies, waits for them, and re-layouts: none -> 17.8 us  [from_root(): return jnp.sum(lax.all_gather(block, axis), axis=0)]
    reduce_sum x0 -> x2, other arithmetic: none -> 17 us  [from_root(): return jnp.sum(lax.all_gather(block, axis), axis=0)]
    unnamed x12 -> x15, local copies, waits for them, and re-layouts: 11.9 us -> 9.69 us
  transfers between devices with their start and end apart: 5 -> 6, of which waited for: 3 -> 5; matrix products, arithmetic and copies ran while one was open for 7% -> 12% of each run, Pallas kernels for 0% -> 0%
where the time goes in v1:
time: 326 us; the launch traced here: 325 us
  waiting for transfers between devices  194 us (60%)
  local copies, waits for them, and re-layouts  40.9 us (13%)
  other arithmetic  33.9 us (10%)
  matrix products  22.7 us (7%)
  between operations  18.7 us (6%)
  starting transfers between devices  14.9 us (5%)
    all_to_all x1, waiting for transfers between devices, on_device(): lax.all_to_all(numerators[None], 'ctx', split_axis=2, concat_axis=0, tile...  90.4 us
    all_gather x2, waiting for transfers between devices, from_root(): return jnp.sum(lax.all_gather(block, axis), axis=0)  51.9 us
    all_gather x1, waiting for transfers between devices, on_device(): all_heads = lax.all_gather(queries, 'ctx', axis=1, tiled=True)  45.4 us
    all_gather x2, local copies, waits for them, and re-layouts, from_root(): return jnp.sum(lax.all_gather(block, axis), axis=0)  17.8 us
    reduce_sum x2, other arithmetic, from_root(): return jnp.sum(lax.all_gather(block, axis), axis=0)  17 us
    dot_general x4, matrix products, partial_value(): jnp.einsum('qhw,kw->qhk', query_block, key_rows, preferred_element_type=j...  13.4 us
    unnamed x15, local copies, waits for them, and re-layouts  9.69 us
    dot_general x4, matrix products, partial_value(): jnp.einsum('qhk,kl->qhl', weights, value_rows, preferred_element_type=jnp...  9.28 us
  transfers between devices with their start and end apart: 6, of which 5 were waited for; matrix products, arithmetic and copies ran while one was open for 12% of the time, Pallas kernels for 0%

profile of v1, /device:TPU:0, one launch (start us, length us, event | category | flops | bytes accessed | tf_op | source)
XLA Modules:
  0.0 325.3 jit_solution(10822426197529073168)
XLA Ops:
  7.3 1.4 fusion.20
  14.1 3.7 %dynamic-slice_select_fusion.1 = (bf16[1024,576]{0,1:T(8,128)(2,1)}, bf16[1024,576]{0,1:T(8,128)(2,1)}) fusion(bf16[4096,576]{0,1:T(8,128)(2,1)} %param.6, s32[]{:T(128)S(6)} %select_n.48, pred[]{:T(512)S(6)} %eq.9, s32[]{:T(128)S(6)} %select_n.53, pred[]{:T(512)S(6)} %eq.10), kind=kLoop, calls=%fused_computation.28 | loop fusion | flops 1179648 | bytes 4718602 | tf_op jit(solution)/shard_map/jit(_where)/select_n | solution.py:15
  18.7 45.4 %all-gather.6.cloned.1.call-done = bf16[16,73728]{1,0:T(8,128)(2,1)} async-done(((bf16[16,9216]{1,0:T(8,128)(2,1)}), bf16[16,73728]{1,0:T(8,128)(2,1)}) %all-gather.6.cloned.1.call-update) | async-done | bytes 2359312 | tf_op jit(solution)/shard_map/all_gather | solution.py:38
  64.1 4.4 %reshape.58 = bf16[4,4,128,576]{3,2,1,0:T(8,128)(2,1)S(1)} reshape(bf16[16,73728]{1,0:T(8,128)(2,1)} %all-gather.6.cloned.1.call-done) | data formatting | bytes 4718592 | tf_op jit(solution)/shard_map/reshape | solution.py:40
  68.5 2.6 copy.24
  71.1 30.6 %all-gather.8.cloned.1.call-done = bf16[4096,576]{0,1:T(8,128)(2,1)} async-done(((bf16[1024,576]{0,1:T(8,128)(2,1)}), bf16[4096,576]{0,1:T(8,128)(2,1)}) %all-gather.8.cloned.1.call-update) | async-done | bytes 4718608 | tf_op jit(solution)/shard_map/all_gather | solution.py:16
  101.7 8.9 %reshape.59 = bf16[4,1024,576]{1,0,2:T(4,128)(2,1)} reshape(bf16[4096,576]{0,1:T(8,128)(2,1)} %all-gather.8.cloned.1.call-done) | data formatting | bytes 9437184 | tf_op jit(solution)/shard_map/all_gather | solution.py:16
  110.5 8.9 %reduce_sum.51 = bf16[1024,576]{0,1:T(8,128)(2,1)S(1)} reduce(bf16[4,1024,576]{1,0,2:T(4,128)(2,1)} %reshape.59, bf16[]{:T(256)} %constant.81.clone.1), dimensions={0}, to_apply=%region_0.1 | reduce | flops 1769472 | bytes 5898242 | tf_op jit(solution)/shard_map/reduce_sum | solution.py:16
  119.4 21.3 %all-gather.10.cloned.1.call-done = bf16[4096,576]{0,1:T(8,128)(2,1)} async-done(((bf16[1024,576]{0,1:T(8,128)(2,1)}), bf16[4096,576]{0,1:T(8,128)(2,1)}) %all-gather.10.cloned.1.call-update) | async-done | bytes 4718608 | tf_op jit(solution)/shard_map/all_gather | solution.py:16
  140.7 8.9 %reshape.60 = bf16[4,1024,576]{1,0,2:T(4,128)(2,1)} reshape(bf16[4096,576]{0,1:T(8,128)(2,1)} %all-gather.10.cloned.1.call-done) | data formatting | bytes 9437184 | tf_op jit(solution)/shard_map/all_gather | solution.py:16
  149.6 8.1 %reduce_sum.52 = bf16[1024,576]{0,1:T(8,128)(2,1)S(1)} reduce(bf16[4,1024,576]{1,0,2:T(4,128)(2,1)} %reshape.60, bf16[]{:T(256)} %constant.81.clone.1), dimensions={0}, to_apply=%region_1.2 | reduce | flops 1769472 | bytes 5898242 | tf_op jit(solution)/shard_map/reduce_sum | solution.py:16
  158.7 1.5 fusion.18
  160.2 1.5 pad_maximum_fusion
  161.7 3.9 %copy.30 = bf16[2048,512]{1,0:T(8,128)(2,1)} copy(bf16[2048,512]{0,1:T(8,128)(2,1)} %fusion.18) | data formatting | bytes 4194304
  165.6 27.9 %while.15 = (s32[]{:T(128)}, f32[4,4,128,512]{3,2,1,0:T(8,128)}, f32[4,4,128]{2,1,0:T(4,128)S(1)}, f32[4,4,128]{2,1,0:T(4,128)S(1)}, s32[4,4]{1,0:T(4,128)S(1)},...) while((s32[]{:T(128)}, f32[4,4,128,512]{3,2,1,0:T(8,128)}, ...), condition=%wide.region_5.6_spmd.clone, body=%wide.region_2.5_spmd.clone.sunk | while | flops 2295342080 | bytes 27149504 | solution.py:59
  165.8 3.4 %select_reduce_fusion.2 = (f32[4,128]{1,0:T(4,128)S(1)}, f32[4,128,2048]{2,1,0:T(8,128)S(1)}) fusion(pred[4,2048]{1,0:T(4,128)(4,1)S(1)} %broadcast_compare_fusion.2, bf16[2048,576]{0,1:T(8,128)(2,1)S(1)} %get-tuple-element.240, bf16[4,4,128,576]{2,3,1,0:T(8,128)(2,1)} %get-tuple-element.239, s32[]{:T(128)} %get-tuple-element.224), kind=kOutput, calls=%fused_computation.3.clone.1 | convolution fusion | flops 1211104768 | bytes 7154176 | tf_op jit(solution)/shard_map/while/body/eval_jaxpr/qhw,kw->qhk/dot_general | solution.py:46
  169.1 1.1 convert_reduce_fusion.2
  170.2 2.3 fusion.26
  172.7 3.4 %select_reduce_fusion.2 = (f32[4,128]{1,0:T(4,128)S(1)}, f32[4,128,2048]{2,1,0:T(8,128)S(1)}) fusion(pred[4,2048]{1,0:T(4,128)(4,1)S(1)} %broadcast_compare_fusion.2, bf16[2048,576]{0,1:T(8,128)(2,1)S(1)} %get-tuple-element.240, bf16[4,4,128,576]{2,3,1,0:T(8,128)(2,1)} %get-tuple-element.239, s32[]{:T(128)} %get-tuple-element.224), kind=kOutput, calls=%fused_computation.3.clone.1 | convolution fusion | flops 1211104768 | bytes 7154176 | tf_op jit(solution)/shard_map/while/body/eval_jaxpr/qhw,kw->qhk/dot_general | solution.py:46
  176.1 1.1 convert_reduce_fusion.2
  177.2 2.3 fusion.26
  179.7 3.4 %select_reduce_fusion.2 = (f32[4,128]{1,0:T(4,128)S(1)}, f32[4,128,2048]{2,1,0:T(8,128)S(1)}) fusion(pred[4,2048]{1,0:T(4,128)(4,1)S(1)} %broadcast_compare_fusion.2, bf16[2048,576]{0,1:T(8,128)(2,1)S(1)} %get-tuple-element.240, bf16[4,4,128,576]{2,3,1,0:T(8,128)(2,1)} %get-tuple-element.239, s32[]{:T(128)} %get-tuple-element.224), kind=kOutput, calls=%fused_computation.3.clone.1 | convolution fusion | flops 1211104768 | bytes 7154176 | tf_op jit(solution)/shard_map/while/body/eval_jaxpr/qhw,kw->qhk/dot_general | solution.py:46
  184.2 2.3 fusion.26
  186.7 3.4 %select_reduce_fusion.2 = (f32[4,128]{1,0:T(4,128)S(1)}, f32[4,128,2048]{2,1,0:T(8,128)S(1)}) fusion(pred[4,2048]{1,0:T(4,128)(4,1)S(1)} %broadcast_compare_fusion.2, bf16[2048,576]{0,1:T(8,128)(2,1)S(1)} %get-tuple-element.240, bf16[4,4,128,576]{2,3,1,0:T(8,128)(2,1)} %get-tuple-element.239, s32[]{:T(128)} %get-tuple-element.224), kind=kOutput, calls=%fused_computation.3.clone.1 | convolution fusion | flops 1211104768 | bytes 7154176 | tf_op jit(solution)/shard_map/while/body/eval_jaxpr/qhw,kw->qhk/dot_general | solution.py:46
  191.2 2.3 fusion.26
  195.5 5.5 %all-to-all-start.1 = ((f32[8,1,256]{2,1,0:T(1,128)}), f32[8,1,256]{2,1,0:T(1,128)S(1)}, u32[]{:S(2)}, u32[]{:S(2)}) async-start(f32[8,1,256]{2,1,0:T(1,128)} %reshape.63), calls=%async_computation.1 | async-start | bytes 16384 | tf_op jit(solution)/shard_map/all_to_all | solution.py:65
  202.5 5.0 %all-to-all-done.1 = f32[8,1,256]{2,1,0:T(1,128)S(1)} async-done(((f32[8,1,256]{2,1,0:T(1,128)}), f32[8,1,256]{2,1,0:T(1,128)S(1)}, u32[]{:S(2)}, u32[]{:S(2)}) %all-to-all-start.1) | async-done | bytes 8224 | tf_op jit(solution)/shard_map/all_to_all | solution.py:65
  207.5 3.6 %all-to-all-start.2 = ((f32[8,1,256]{2,1,0:T(1,128)}), f32[8,1,256]{2,1,0:T(1,128)S(1)}, u32[]{:S(2)}, u32[]{:S(2)}) async-start(f32[8,1,256]{2,1,0:T(1,128)} %reshape.65), calls=%async_computation.2 | async-start | bytes 16384 | tf_op jit(solution)/shard_map/all_to_all | solution.py:66
  211.1 6.5 %copy.29 = f32[1,16,128,512]{3,1,0,2:T(8,128)} copy(f32[1,16,128,512]{3,2,1,0:T(8,128)} %bitcast.2) | data formatting | bytes 8388608 | tf_op jit(solution)/shard_map/broadcast_in_dim;reshape | solution.py:64
  217.6 5.7 %all-to-all-start = ((f32[1,16,128,512]{3,1,0,2:T(8,128)}), f32[1,16,128,512]{3,1,0,2:T(8,128)}, u32[]{:S(2)}, u32[]{:S(2)}) async-start(f32[1,16,128,512]{3,1,0,2:T(8,128)} %copy.29), calls=%async_computation | async-start | bytes 8388608 | tf_op jit(solution)/shard_map/all_to_all | solution.py:64
  224.9 90.4 %all-to-all-done = f32[1,16,128,512]{3,1,0,2:T(8,128)} async-done(((f32[1,16,128,512]{3,1,0,2:T(8,128)}), f32[1,16,128,512]{3,1,0,2:T(8,128)}, u32[]{:S(2)}, u32[]{:S(2)}) %all-to-all-start) | async-done | bytes 4194336 | tf_op jit(solution)/shard_map/all_to_all | solution.py:64
  315.3 2.6 multiply_reduce_fusion
  (65 shorter events, 11.4 us)
Async XLA Ops:
  6.5 12.2 %copy-start.3 = (s32[2]{0:T(128)S(1)}, s32[2]{0:T(128)}, u32[]{:S(2)}) copy-start(s32[2]{0:T(128)} %param.8) | copy-start | bytes 28
  6.5 12.1 %copy-start.4 = (s32[16]{0:T(128)S(1)}, s32[16]{0:T(128)}, u32[]{:S(2)}) copy-start(s32[16]{0:T(128)} %param.9) | copy-start | bytes 196
  6.5 57.6 %all-gather.6.cloned.1.call-start = ((), (), s32[]{:S(2)}) async-start(), calls=%async_computation.3 | async-start | bytes 2654208 | tf_op jit(solution)/shard_map/all_gather | solution.py:38
  7.3 94.4 %all-gather.8.cloned.1.call-start = ((), (), s32[]{:S(2)}) async-start(), calls=%async_computation.4 | async-start | bytes 5898240 | tf_op jit(solution)/shard_map/all_gather | solution.py:16
  17.8 122.9 %all-gather.10.cloned.1.call-start = ((), (), s32[]{:S(2)}) async-start(), calls=%async_computation.5 | async-start | bytes 5898240 | tf_op jit(solution)/shard_map/all_gather | solution.py:16
  157.7 1.0 copy-start
  161.6 4.0 %copy-start.2 = (f32[4,4,128]{2,1,0:T(4,128)S(1)}, f32[4,4,128]{2,1,0:T(4,128)}, u32[]{:S(2)}) copy-start(f32[4,4,128]{2,1,0:T(4,128)} %custom-call.2) | copy-start | bytes 24580
  165.8 4.5 %copy-start.1 = (bf16[2048,512]{1,0:T(8,128)(2,1)S(1)}, bf16[2048,512]{1,0:T(8,128)(2,1)}, u32[]{:S(2)}) copy-start(bf16[2048,512]{1,0:T(8,128)(2,1)} %get-tuple-element.241) | copy-start | bytes 6291460 | tf_op jit(solution)/shard_map/while
  172.7 4.5 %copy-start.1 = (bf16[2048,512]{1,0:T(8,128)(2,1)S(1)}, bf16[2048,512]{1,0:T(8,128)(2,1)}, u32[]{:S(2)}) copy-start(bf16[2048,512]{1,0:T(8,128)(2,1)} %get-tuple-element.241) | copy-start | bytes 6291460 | tf_op jit(solution)/shard_map/while
  179.7 4.5 %copy-start.1 = (bf16[2048,512]{1,0:T(8,128)(2,1)S(1)}, bf16[2048,512]{1,0:T(8,128)(2,1)}, u32[]{:S(2)}) copy-start(bf16[2048,512]{1,0:T(8,128)(2,1)} %get-tuple-element.241) | copy-start | bytes 6291460 | tf_op jit(solution)/shard_map/while
  186.7 4.5 %copy-start.1 = (bf16[2048,512]{1,0:T(8,128)(2,1)S(1)}, bf16[2048,512]{1,0:T(8,128)(2,1)}, u32[]{:S(2)}) copy-start(bf16[2048,512]{1,0:T(8,128)(2,1)} %get-tuple-element.241) | copy-start | bytes 6291460 | tf_op jit(solution)/shard_map/while
  195.5 12.0 %all-to-all-start.1 = ((f32[8,1,256]{2,1,0:T(1,128)}), f32[8,1,256]{2,1,0:T(1,128)S(1)}, u32[]{:S(2)}, u32[]{:S(2)}) async-start(f32[8,1,256]{2,1,0:T(1,128)} %reshape.63), calls=%async_computation.1 | async-start | bytes 16384 | tf_op jit(solution)/shard_map/all_to_all | solution.py:65
  207.5 10.1 %all-to-all-start.2 = ((f32[8,1,256]{2,1,0:T(1,128)}), f32[8,1,256]{2,1,0:T(1,128)S(1)}, u32[]{:S(2)}, u32[]{:S(2)}) async-start(f32[8,1,256]{2,1,0:T(1,128)} %reshape.65), calls=%async_computation.2 | async-start | bytes 16384 | tf_op jit(solution)/shard_map/all_to_all | solution.py:66
  217.6 97.7 %all-to-all-start = ((f32[1,16,128,512]{3,1,0,2:T(8,128)}), f32[1,16,128,512]{3,1,0,2:T(8,128)}, u32[]{:S(2)}, u32[]{:S(2)}) async-start(f32[1,16,128,512]{3,1,0,2:T(8,128)} %copy.29), calls=%async_computation | async-start | bytes 8388608 | tf_op jit(solution)/shard_map/all_to_all | solution.py:64
Sparse Core Ops, SparseCore 0:
  9.5 54.5 all-gather.5
  65.7 35.9 all-gather.7
  103.2 37.4 all-gather.9
